TPU v7x, 768 devices: a whole 4x8x12 slice. The times are simulated.
768 devices in a mesh: space: 32 (over y, x), tm: 24 (over z, core).
Axes of the slice: x: 4, y: 8, z: 12, core: 2. Of those that a mesh axis runs over, the one named last changes fastest.
Arguments:
- links: float32 [24, 3, 2, 3, 3, 64, 4096], P('tm', None, None, None, None, 'space'), may hold values from -1 to 1, as said below
- propagator: float32 [2, 144, 64, 4096], P(None, 'tm', 'space'), may hold values from -6 to 6
- sink_time: int32 [1], replicated, may hold values from 0 to 98303
- src_time: int32 [1], replicated, may hold values from 0 to 98303
- src_site: int32 [1], replicated, may hold values from 0 to 262143
Outputs:
- fixed_links: float32 [24, 3, 2, 3, 3, 64, 4096], P('tm', None, None, None, None, 'space')
- wall: float32 [2, 144], replicated
Inputs may be any that keep to these rules, and one draw needn't show every extreme that they name: `links`: every link is a special unitary 3 x 3 matrix up to rounding.
All inputs are finite; a program needn't handle non-finite values.
Results may differ from a plain program's by a relative error of at most 0.0001.
Values sent between devices are 32-bit elements; how exact they have to be, the bound alone decides.
A program may use at most 128 MiB of HBM per device.

v0:
```python
import math

import jax
import jax.numpy as jnp
from jax import lax
from jax.sharding import Mesh
from jax.sharding import PartitionSpec as P

L = 64
SC = 12
ITERS = 2
SPACE = ("space_0", "space_1")
TM = ("tm_0", "tm_1")
SPACE_TM = ("space_0", "space_1", "tm_0", "tm_1")


STEP_SIZE = 0.08
PEAK_SQUARE = 12.0
ENTRY_PAIRS = ((0, 0), (0, 1), (0, 2), (1, 1), (1, 2), (2, 2))
EXACT = lax.Precision.HIGHEST


def from_behind(value, axis, by):
    size = lax.axis_size(axis)
    return lax.ppermute(value, axis, [(i, (i + by) % size) for i in range(size)])


def picked_2(value, axis, root):
    return lax.dynamic_index_in_dim(lax.all_gather(value, axis), root, 0, keepdims=False)


def over_axes(value, axes):
    for axis in axes:
        value = lax.psum(value, axis)
    return value


def colour_product(left_matrix, right_matrix):
    return jnp.sum(left_matrix[:, :, None] * right_matrix[None, :, :], axis=1)


def complex_product(left_matrix, right_matrix):
    real_part = colour_product(left_matrix[0], right_matrix[0]) - colour_product(
        left_matrix[1], right_matrix[1]
    )
    imag_part = colour_product(left_matrix[0], right_matrix[1]) + colour_product(
        left_matrix[1], right_matrix[0]
    )
    return jnp.stack([real_part, imag_part])


def dagger(matrix):
    return jnp.stack([jnp.swapaxes(matrix[0], 0, 1), -jnp.swapaxes(matrix[1], 0, 1)])


def roll_depth(values, amount):
    old_shape = values.shape
    folded = values.reshape(old_shape[:-1] + (L, L))
    return jnp.roll(folded, amount, axis=-1).reshape(old_shape)


def project(divergence):
    real_part = 0.5 * (divergence[0] - jnp.swapaxes(divergence[0], 0, 1))
    imag_part = 0.5 * (divergence[1] + jnp.swapaxes(divergence[1], 0, 1))
    trace_third = (imag_part[0, 0] + imag_part[1, 1] + imag_part[2, 2]) / 3.0
    real_six = jnp.stack(
        [real_part[row_index, column_index] for row_index, column_index in ENTRY_PAIRS]
    )
    imag_six = jnp.stack(
        [
            (
                imag_part[row_index, column_index] - trace_third
                if row_index == column_index
                else imag_part[row_index, column_index]
            )
            for row_index, column_index in ENTRY_PAIRS
        ]
    )
    return (real_six, imag_six)


def assemble(real_six, imag_six):
    zero_plane = jnp.zeros_like(real_six[0])
    position = {}
    for entry_index, entry_pair in enumerate(ENTRY_PAIRS):
        position[entry_pair] = entry_index
    real_rows = []
    imag_rows = []
    for row_index in range(3):
        real_line = []
        imag_line = []
        for column_index in range(3):
            if row_index == column_index:
                real_line.append(zero_plane)
                imag_line.append(imag_six[position[row_index, row_index]])
            elif row_index < column_index:
                slot_index = position[row_index, column_index]
                real_line.append(real_six[slot_index])
                imag_line.append(imag_six[slot_index])
            else:
                slot_index = position[column_index, row_index]
                real_line.append(-real_six[slot_index])
                imag_line.append(imag_six[slot_index])
        real_rows.append(jnp.stack(real_line))
        imag_rows.append(jnp.stack(imag_line))
    return jnp.stack([jnp.stack(real_rows), jnp.stack(imag_rows)])


def exponential(algebra):
    unit_matrix = jnp.eye(3, dtype=jnp.float32).reshape((3, 3) + (1,) * (algebra.ndim - 3))
    identity = jnp.stack(
        [
            jnp.broadcast_to(unit_matrix, algebra.shape[1:]),
            jnp.zeros(algebra.shape[1:], jnp.float32),
        ]
    )
    result = identity
    for degree in range(6, 0, -1):
        result = identity + complex_product(algebra, result) / degree
    for square_index in range(3):
        result = complex_product(result, result)
    return result


def rotate(lattice, gauge_field, gauge_ahead):
    along_x = complex_product(complex_product(gauge_field, lattice[0]), dagger(gauge_ahead))
    along_y = complex_product(
        complex_product(gauge_field, lattice[1]), dagger(jnp.roll(gauge_field, -L, axis=4))
    )
    along_z = complex_product(
        complex_product(gauge_field, lattice[2]), dagger(roll_depth(gauge_field, -1))
    )
    return jnp.stack([along_x, along_y, along_z])


def sink_product(gauge_field, propagator):
    pair_count = propagator.shape[1]
    source = propagator.reshape((2, pair_count // 3, 3) + propagator.shape[2:])
    pattern = "acxn,qcxn->qa"
    real_part = jnp.einsum(pattern, gauge_field[0], source[0], precision=EXACT) - jnp.einsum(
        pattern, gauge_field[1], source[1], precision=EXACT
    )
    imag_part = jnp.einsum(pattern, gauge_field[0], source[1], precision=EXACT) + jnp.einsum(
        pattern, gauge_field[1], source[0], precision=EXACT
    )
    return jnp.stack([real_part.reshape(pair_count), imag_part.reshape(pair_count)])


def source_rotate(wall_total, anchor):
    by_spin = wall_total.reshape(2, 4, 3, SC)
    pattern = "scn,bc->sbn"
    real_part = jnp.einsum(pattern, by_spin[0], anchor[0], precision=EXACT) + jnp.einsum(
        pattern, by_spin[1], anchor[1], precision=EXACT
    )
    imag_part = jnp.einsum(pattern, by_spin[1], anchor[0], precision=EXACT) - jnp.einsum(
        pattern, by_spin[0], anchor[1], precision=EXACT
    )
    return jnp.stack([real_part.reshape(SC * SC), imag_part.reshape(SC * SC)])


def phase_tables(length):
    wavenumber = jnp.arange(length, dtype=jnp.int32)
    phase_index = wavenumber[:, None] * wavenumber[None, :] % length
    angles = phase_index.astype(jnp.float32) * (2.0 * math.pi / length)
    return (jnp.cos(angles), jnp.sin(angles))


def sine_squares(length):
    wavenumber = jnp.arange(length, dtype=jnp.float32)
    return 4.0 * jnp.sin(math.pi * wavenumber / length) ** 2


def transform(real_part, imag_part, pattern, inverse, cosine_table, sine_table):
    cosine_real = jnp.einsum(pattern, cosine_table, real_part, precision=EXACT)
    cosine_imag = jnp.einsum(pattern, cosine_table, imag_part, precision=EXACT)
    sine_real = jnp.einsum(pattern, sine_table, real_part, precision=EXACT)
    sine_imag = jnp.einsum(pattern, sine_table, imag_part, precision=EXACT)
    if inverse:
        length = cosine_table.shape[0]
        return ((cosine_real - sine_imag) / length, (cosine_imag + sine_real) / length)
    return (cosine_real + sine_imag, cosine_imag - sine_real)


def fetch_lower(along_x):
    planes = along_x.shape[3]
    return from_behind(along_x[:, :, :, planes - 1 : planes], SPACE, 1)


def body(links, propagator, sink_time, src_time, src_site):
    space_count = lax.axis_size(SPACE)
    time_count = lax.axis_size(TM)
    planes = links.shape[5]
    across = planes * space_count
    columns = L * L // space_count
    cosine_table, sine_table = phase_tables(L)
    cosine_across, sine_across = phase_tables(across)
    space_index = lax.axis_index(SPACE)
    corner = space_index * planes
    square_side = sine_squares(L)
    square_flat = (square_side[:, None] + square_side[None, :]).reshape(L * L)
    local_square = lax.dynamic_slice_in_dim(square_flat, space_index * columns, columns)
    momentum = sine_squares(across)[:, None] + local_square[None, :]
    guarded = jnp.where(momentum > 0.0, momentum, 1.0)
    filter_weight = jnp.where(momentum > 0.0, PEAK_SQUARE / guarded, 0.0)[None]
    lattice = links[0]
    overall = None
    for sweep_index in range(ITERS):
        lower_plane = fetch_lower(lattice[0])
        behind = jnp.concatenate([lower_plane, lattice[0][:, :, :, : planes - 1]], axis=3)
        divergence = (
            behind
            - lattice[0]
            + jnp.roll(lattice[1], L, axis=4)
            - lattice[1]
            + roll_depth(lattice[2], 1)
            - lattice[2]
        )
        real_six, imag_six = project(divergence)
        slab_shape = (6, planes, L, L)
        real_six, imag_six = transform(
            real_six.reshape(slab_shape),
            imag_six.reshape(slab_shape),
            "kn,exyn->exyk",
            False,
            cosine_table,
            sine_table,
        )
        real_six, imag_six = transform(
            real_six, imag_six, "kn,exnz->exkz", False, cosine_table, sine_table
        )
        spectrum = jnp.stack(
            [real_six.reshape(6, planes, L * L), imag_six.reshape(6, planes, L * L)]
        )
        turned = lax.all_to_all(spectrum, SPACE, split_axis=3, concat_axis=2, tiled=True)
        real_six, imag_six = transform(
            turned[0], turned[1], "kn,enc->ekc", False, cosine_across, sine_across
        )
        real_six, imag_six = transform(
            real_six * filter_weight,
            imag_six * filter_weight,
            "kn,enc->ekc",
            True,
            cosine_across,
            sine_across,
        )
        filtered = jnp.stack([real_six, imag_six])
        grouped = filtered.reshape(2, 6, space_count, planes, columns)
        onward = jnp.roll(grouped[:, :, :, 0:1], -1, axis=2)
        widened = jnp.concatenate([grouped, onward], axis=3).reshape(
            2, 6, space_count * (planes + 1), columns
        )
        returned = lax.all_to_all(widened, SPACE, split_axis=2, concat_axis=3, tiled=True)
        row_count = planes + 1
        back_shape = (6, row_count, L, L)
        real_six, imag_six = transform(
            returned[0].reshape(back_shape),
            returned[1].reshape(back_shape),
            "kn,exyn->exyk",
            True,
            cosine_table,
            sine_table,
        )
        real_six, imag_six = transform(
            real_six, imag_six, "kn,exnz->exkz", True, cosine_table, sine_table
        )
        algebra = assemble(
            real_six.reshape(6, row_count, L * L), imag_six.reshape(6, row_count, L * L)
        )
        rotation = exponential(algebra * (STEP_SIZE / 16.0))
        gauge_field = rotation[:, :, :, :planes]
        gauge_ahead = rotation[:, :, :, 1:]
        lattice = rotate(lattice, gauge_field, gauge_ahead)
        overall = gauge_field if overall is None else complex_product(gauge_field, overall)
    tm_index = lax.axis_index(TM)
    sink_slice = sink_time[0] % time_count
    source_slice = src_time[0] % time_count
    sink_gauge = picked_2(overall, TM, sink_slice)
    local_wall = sink_product(sink_gauge, propagator)
    pair_count = propagator.shape[1]
    root = jnp.zeros((), jnp.int32)
    padded = lax.dynamic_update_slice(
        jnp.zeros((2, SC * SC), jnp.float32), local_wall, (root, tm_index * pair_count)
    )
    site_index = src_site[0]
    plane_index = site_index // (L * L) - corner
    column_index = site_index % (L * L)
    present = (source_slice == tm_index) & (plane_index >= 0) & (plane_index < planes)
    clamped = jnp.clip(plane_index, 0, planes - 1)
    picked = lax.dynamic_slice(
        overall, (root, root, root, clamped, column_index), (2, 3, 3, 1, 1)
    ).reshape(2, 3, 3)
    local_anchor = jnp.where(present, picked, 0.0)
    wall_total, anchor = (over_axes(padded, SPACE_TM), over_axes(local_anchor, SPACE_TM))
    wall = source_rotate(wall_total, anchor)
    return (lattice[None], wall * float(across * L * L) ** (-0.5))


def solution(mesh):
    torus = Mesh(mesh.devices.reshape(8, 4, 12, 2), ("space_0", "space_1", "tm_0", "tm_1"))
    placed = (P(TM, None, None, None, None, SPACE, None), P(None, TM, SPACE, None), P(), P(), P())
    return jax.shard_map(
        body,
        mesh=torus,
        in_specs=placed,
        out_specs=(P(TM, None, None, None, None, SPACE, None), P()),
        check_vma=False,
    )
```

profile of v0, /device:TPU:1, one launch (start us, length us, event | category | flops | bytes accessed | tf_op | source)
XLA Modules:
  0.0 568.3 jit_solution(4258606599826818418)
XLA Ops:
  7.2 1.5 fusion.425
  10.2 3.9 collective-permute-start
  15.7 1.8 reshape_squeeze.15
  19.3 1.9 reshape.1162
  21.2 1.6 collective-permute-done
  22.7 2.2 fusion.53
  33.5 8.8 %copy.405 = f32[2,6,2,4096]{1,2,0,3:T(2,128)} copy(f32[2,6,2,4096]{3,2,1,0:T(2,128)S(1)} %pad_maximum_fusion.13) | data formatting | bytes 786432 | tf_op jit(solution)/shard_map/stack | solution.py:231
  42.3 15.0 %reshape.1193 = f32[32,1,3072]{2,1,0:T(1,128)} reshape(f32[4096,2,2,6]{3,2,1,0:T(2,128)} %bitcast.697) | data formatting | bytes 786432
  57.3 8.9 %all-to-all-start = ((f32[32,1,3072]{2,1,0:T(1,128)}), f32[32,1,3072]{2,1,0:T(1,128)S(1)}, u32[]{:S(2)}, u32[]{:S(2)}) async-start(f32[32,1,3072]{2,1,0:T(1,128)} %reshape.1193), calls=%async_computation | async-start | bytes 786432 | tf_op jit(solution)/shard_map/all_to_all | solution.py:234
  66.6 11.1 %all-to-all-done = f32[32,1,3072]{2,1,0:T(1,128)S(1)} async-done(((f32[32,1,3072]{2,1,0:T(1,128)}), f32[32,1,3072]{2,1,0:T(1,128)S(1)}, u32[]{:S(2)}, u32[]{:S(2)}) %all-to-all-start) | async-done | bytes 393248 | tf_op jit(solution)/shard_map/all_to_all | solution.py:234
  78.2 1.6 reduce.12
  79.8 14.4 %reshape.1194 = f32[4096,2,2,6]{3,2,1,0:T(2,128)} reshape(f32[32,3072]{1,0:T(8,128)S(1)} %reduce.12) | data formatting | bytes 786432
  94.2 9.8 %copy.406 = f32[2,6,2,32,128]{4,2,3,1,0:T(2,128)S(1)} copy(f32[2,6,2,32,128]{1,2,0,4,3:T(2,128)} %bitcast.698) | data formatting | bytes 786432 | tf_op jit(solution)/shard_map/all_to_all | solution.py:234
  109.4 4.0 all-to-all-start.1
  114.9 11.9 %all-to-all-done.1 = f32[2,6,96,128]{3,0,1,2:T(2,128)S(1)} async-done(((f32[2,6,96,128]{3,0,1,2:T(2,128)}), f32[2,6,96,128]{3,0,1,2:T(2,128)S(1)}, u32[]{:S(2)}, u32[]{:S(2)}) %all-to-all-start.1) | async-done | bytes 589856 | tf_op jit(solution)/shard_map/all_to_all | solution.py:252
  143.2 1.9 multiply_reduce_fusion.64
  146.1 1.9 multiply_reduce_fusion.60
  148.9 1.9 multiply_reduce_fusion.56
  152.3 1.9 multiply_reduce_fusion.52
  155.1 1.9 multiply_reduce_fusion.48
  157.9 1.7 multiply_reduce_fusion.41
  159.9 1.7 multiply_reduce_fusion.37
  162.0 1.7 multiply_reduce_fusion.34
  171.1 1.8 copy.568
  175.0 13.7 %multiply_reduce_fusion.115 = (f32[3,3,2,4096]{3,2,1,0:T(2,128)}, f32[3,3,2,4096]{3,2,1,0:T(2,128)}, f32[3,3,2,4096]{3,2,1,0:T(2,128)}, f32[3,3,2,4096]{3,2,1,0:...) fusion(f32[3,3,2,4096]{3,2,1,0:T(2,128)S(1)} %get-tuple-element, ...), kind=kLoop, calls=%fused_computation.218 | loop fusion | flops 4423680 | bytes 5898240 | tf_op jit(solution)/shard_map/reduce_sum | solution.py:39
  189.6 1.9 multiply_reduce_fusion.96
  194.2 1.9 multiply_reduce_fusion.114
  197.9 2.6 collective-permute-start.1
  205.0 1.9 multiply_reduce_fusion.106
  209.0 2.5 fusion.37
  217.4 1.6 fusion.12
  218.9 1.6 fusion.13
  223.4 8.3 %copy.443 = f32[2,6,2,4096]{1,2,0,3:T(2,128)} copy(f32[2,6,2,4096]{3,2,1,0:T(2,128)S(1)} %pad_maximum_fusion.14) | data formatting | bytes 786432 | tf_op jit(solution)/shard_map/stack | solution.py:231
  231.8 14.4 %reshape.1195 = f32[32,1,3072]{2,1,0:T(1,128)S(1)} reshape(f32[4096,2,2,6]{3,2,1,0:T(2,128)} %bitcast.699) | data formatting | bytes 786432
  246.1 16.6 %all_to_all.60 = f32[32,1,3072]{2,1,0:T(1,128)S(1)} all-to-all(f32[32,1,3072]{2,1,0:T(1,128)S(1)} %reshape.1195), channel_id=1, replica_groups=mesh['space_0'=8,'space_1'=4,'tm_0'=12,'tm_1'=2] {'space_0','space_1'}, dimensions={0} | all-to-all | bytes 786432 | tf_op jit(solution)/shard_map/all_to_all | solution.py:234
  262.7 1.6 reduce.13
  264.3 14.4 %reshape.1196 = f32[4096,2,2,6]{3,2,1,0:T(2,128)} reshape(f32[32,3072]{1,0:T(8,128)S(1)} %reduce.13) | data formatting | bytes 786432
  278.8 9.8 %copy.444 = f32[2,6,2,32,128]{4,2,3,1,0:T(2,128)S(1)} copy(f32[2,6,2,32,128]{1,2,0,4,3:T(2,128)} %bitcast.700) | data formatting | bytes 786432 | tf_op jit(solution)/shard_map/all_to_all | solution.py:234
  293.1 16.9 %all_to_all.61 = f32[2,6,96,128]{3,0,1,2:T(2,128)S(1)} all-to-all(f32[2,6,96,128]{3,0,1,2:T(2,128)S(1)} %copy.447), channel_id=1, replica_groups=mesh['space_0'=8,'space_1'=4,'tm_0'=12,'tm_1'=2] {'space_0','space_1'}, dimensions={2} | all-to-all | bytes 1179648 | tf_op jit(solution)/shard_map/all_to_all | solution.py:252
  320.0 1.6 copy.453
  321.6 1.6 slice.802
  337.5 1.9 multiply_reduce_fusion.30
  340.4 1.9 multiply_reduce_fusion.26
  343.2 1.9 multiply_reduce_fusion.22
  346.1 2.1 multiply_reduce_fusion.18
  349.1 1.9 multiply_reduce_fusion.14
  351.9 1.7 multiply_reduce_fusion.7
  354.0 1.7 multiply_reduce_fusion.3
  356.0 1.7 multiply_reduce_fusion
  360.5 10.6 %multiply_reduce_fusion.70 = (f32[3,3,2,4096]{3,2,1,0:T(2,128)S(1)}, f32[3,3,2,4096]{3,2,1,0:T(2,128)}, f32[3,3,2,4096]{3,2,1,0:T(2,128)}, f32[3,3,2,4096]{3,2,1...) fusion(f32[3,3,2,4096]{3,2,1,0:T(2,128)S(1)} %copy-done.6, ...), kind=kLoop, calls=%fused_computation.173 | loop fusion | flops 5898240 | bytes 7667712 | tf_op jit(solution)/shard_map/reduce_sum | solution.py:39
  383.3 1.9 multiply_reduce_fusion.74
  385.2 1.9 multiply_reduce_fusion.90
  388.1 2.1 multiply_reduce_fusion.82
  392.1 2.1 maximum_bitcast_fusion
  394.3 86.5 %all-gather.3.cloned.1.call-done = f32[48,3,3,2,4096]{4,3,2,1,0:T(2,128)} async-done(((f32[2,3,3,2,4096]{4,3,2,1,0:T(2,128)}), f32[48,3,3,2,4096]{4,3,2,1,0:T(2,128)}) %all-gather.3.cloned.1.call-update) | async-done | bytes 14155792 | tf_op jit(solution)/shard_map/all_gather | solution.py:29
  480.8 18.7 %copy.473 = f32[48,3,3,2,4096]{4,1,3,2,0:T(4,128)S(1)} copy(f32[48,3,3,2,4096]{4,3,2,1,0:T(2,128)} %all-gather.3.cloned.1.call-done) | data formatting | bytes 28311552 | tf_op jit(solution)/shard_map/all_gather | solution.py:29
  499.5 1.8 convolution_bitcast_fusion
  501.3 1.8 convolution_bitcast_fusion.2
  503.1 1.9 fusion.33
  505.1 1.8 fusion.31
  507.3 13.6 %all-reduce.2 = (f32[2,144]{1,0:T(2,128)S(1)}, f32[2,3,3]{2,0,1:T(2,128)S(1)}) all-reduce(f32[2,144]{1,0:T(2,128)S(1)} %dynamic_update_slice.3, f32[2,3,3]{2,0,1:T(2,128)S(1)} %bitcast.750), channel_id=1, replica_groups=mesh['space_0'=8,'space_1'=4,'tm_0'=12,'tm_1'=2] {'space_0'}, use_global_device_ids=true, to_apply=%region_128.129 | all-reduce | flops 306 | bytes 2448 | tf_op jit(solution)/shard_map/psum | solution.py:34
  520.9 8.5 %all-reduce.3 = (f32[2,144]{1,0:T(2,128)S(1)}, f32[2,3,3]{2,0,1:T(2,128)S(1)}) all-reduce(f32[2,144]{1,0:T(2,128)S(1)} %get-tuple-element.130, f32[2,3,3]{2,0,1:T(2,128)S(1)} %get-tuple-element.131), channel_id=1, replica_groups=mesh['space_0'=8,'space_1'=4,'tm_0'=12,'tm_1'=2] {'space_1'}, use_global_device_ids=true, to_apply=%region_129.130 | all-reduce | flops 306 | bytes 2448 | tf_op jit(solution)/shard_map/psum | solution.py:34
  529.4 17.5 %all-reduce.1 = (f32[2,144]{1,0:T(2,128)S(1)}, f32[2,3,3]{2,0,1:T(2,128)S(1)}) all-reduce(f32[2,144]{1,0:T(2,128)S(1)} %get-tuple-element.132, f32[2,3,3]{2,0,1:T(2,128)S(1)} %get-tuple-element.133), channel_id=1, replica_groups=mesh['space_0'=8,'space_1'=4,'tm_0'=12,'tm_1'=2] {'tm_0'}, use_global_device_ids=true, to_apply=%region_130.131 | all-reduce | flops 306 | bytes 2448 | tf_op jit(solution)/shard_map/psum | solution.py:34
  546.9 12.8 %all-reduce.4 = (f32[2,144]{1,0:T(2,128)S(1)}, f32[2,3,3]{2,0,1:T(2,128)S(1)}) all-reduce(f32[2,144]{1,0:T(2,128)S(1)} %get-tuple-element.128, f32[2,3,3]{2,0,1:T(2,128)S(1)} %get-tuple-element.129), channel_id=1, replica_groups=mesh['space_0'=8,'space_1'=4,'tm_0'=12,'tm_1'=2] {'tm_1'}, use_global_device_ids=true, to_apply=%region_131.132 | all-reduce | flops 306 | bytes 2448 | tf_op jit(solution)/shard_map/psum | solution.py:34
  (455 shorter events, 123.5 us)
Async XLA Ops:
  10.2 12.5 %collective-permute-start = (f32[2,3,3,1,4096]{4,3,1,2,0:T(1,128)}, f32[2,3,3,1,4096]{4,3,1,2,0:T(1,128)}, u32[]{:S(2)}, u32[]{:S(2)}) collective-permute-start(f32[2,3,3,1,4096]{4,3,1,2,0:T(1,128)} %get-tuple-element.217), channel_id=1, source_target_pairs={{0,24},{24,48},{48,72},{72,96},{96,120},{120,144},{144,168},{168,1... | collective-permute-start | bytes 884744 | tf_op jit(solution)/shard_map/ppermute | solution.py:25
  19.3 3.5 copy-start.28
  19.3 3.5 copy-start.47
  57.3 20.4 %all-to-all-start = ((f32[32,1,3072]{2,1,0:T(1,128)}), f32[32,1,3072]{2,1,0:T(1,128)S(1)}, u32[]{:S(2)}, u32[]{:S(2)}) async-start(f32[32,1,3072]{2,1,0:T(1,128)} %reshape.1193), calls=%async_computation | async-start | bytes 786432 | tf_op jit(solution)/shard_map/all_to_all | solution.py:234
  66.6 38.9 %copy-start.37 = (f32[64,128]{1,0:T(8,128)}, f32[64,128]{1,0:T(8,128)S(1)}, u32[]{:S(2)}) copy-start(f32[64,128]{1,0:T(8,128)S(1)} %fusion.84) | copy-start | bytes 98308
  107.8 5.8 %copy-start = (f32[1,3,2,3,3,2,4096]{6,5,4,3,2,1,0:T(2,128)S(1)}, f32[1,3,2,3,3,2,4096]{6,5,4,3,2,1,0:T(2,128)}, u32[]{:S(2)}) copy-start(f32[1,3,2,3,3,2,4096]{6,5,4,3,2,1,0:T(2,128)} %param.5) | copy-start | bytes 5308420
  109.4 17.4 %all-to-all-start.1 = ((f32[2,6,96,128]{3,0,1,2:T(2,128)}), f32[2,6,96,128]{3,0,1,2:T(2,128)S(1)}, u32[]{:S(2)}, u32[]{:S(2)}) async-start(f32[2,6,96,128]{3,0,1,2:T(2,128)} %copy.409), calls=%async_computation.1 | async-start | bytes 1179648 | tf_op jit(solution)/shard_map/all_to_all | solution.py:252
  113.4 367.4 %all-gather.3.cloned.1.call-start = ((), (), s32[]{:S(2)}) async-start(), calls=%async_computation.4 | async-start | bytes 14745600 | tf_op jit(solution)/shard_map/all_gather | solution.py:29
  137.7 0.8 copy-start.39
  167.6 7.3 %copy-start.5 = (f32[3,3,2,4096]{3,2,1,0:T(2,128)}, f32[3,3,2,4096]{3,2,1,0:T(2,128)S(1)}, u32[]{:S(2)}) copy-start(f32[3,3,2,4096]{3,2,1,0:T(2,128)S(1)} %get-tuple-element.203) | copy-start | bytes 884740
  168.6 6.3 %copy-start.7 = (f32[3,3,2,4096]{3,2,1,0:T(2,128)}, f32[3,3,2,4096]{3,2,1,0:T(2,128)S(1)}, u32[]{:S(2)}) copy-start(f32[3,3,2,4096]{3,2,1,0:T(2,128)S(1)} %get-tuple-element.201) | copy-start | bytes 884740
  170.1 4.8 copy-start.12
  170.1 4.8 copy-start.13
  170.1 4.8 copy-start.14
  170.1 4.8 copy-start.15
  171.1 3.8 copy-start.16
  171.1 3.8 copy-start.17
  188.7 1.0 copy-start.22
  192.1 1.8 copy-start.20
  192.1 1.8 copy-start.21
  192.7 1.5 copy-start.25
  192.7 1.5 copy-start.26
  196.2 4.7 copy-start.1
  196.4 4.5 copy-start.3
  197.9 11.1 %collective-permute-start.1 = (f32[2,3,3,1,4096]{4,3,2,1,0:T(1,128)}, f32[2,3,3,1,4096]{4,3,2,1,0:T(1,128)}, u32[]{:S(2)}, u32[]{:S(2)}) collective-permute-start(f32[2,3,3,1,4096]{4,3,2,1,0:T(1,128)} %get-tuple-element.198), channel_id=1, source_target_pairs={{0,24},{24,48},{48,72},{72,96},{96,120},{120,144},{144,168},{168,1... | collective-permute-start | bytes 884744 | tf_op jit(solution)/shard_map/ppermute | solution.py:25
  201.3 1.1 copy-start.9
  202.4 2.4 copy-start.18
  202.4 2.4 copy-start.19
  206.9 2.1 copy-start.2
  206.9 2.1 copy-start.4
  206.9 2.1 copy-start.27
  278.8 10.8 %copy-start.38 = (f32[64,128]{1,0:T(8,128)S(1)}, f32[64,128]{1,0:T(8,128)}, u32[]{:S(2)}) copy-start(f32[64,128]{1,0:T(8,128)} %copy-done.37) | copy-start | bytes 98308
  324.4 5.9 %copy-start.44 = (f32[1,3,64,64]{2,3,1,0:T(8,128)S(1)}, f32[1,3,64,64]{2,3,1,0:T(8,128)}, u32[]{:S(2)}) copy-start(f32[1,3,64,64]{2,3,1,0:T(8,128)} %get-tuple-element.186) | copy-start | bytes 147460
  324.4 6.2 %copy-start.43 = (f32[1,3,64,64]{2,3,1,0:T(8,128)S(1)}, f32[1,3,64,64]{2,3,1,0:T(8,128)}, u32[]{:S(2)}) copy-start(f32[1,3,64,64]{2,3,1,0:T(8,128)} %get-tuple-element.187) | copy-start | bytes 147460
  324.4 6.4 %copy-start.40 = (f32[1,3,4096]{2,0,1:T(1,128)S(1)}, f32[1,3,4096]{2,0,1:T(1,128)}, u32[]{:S(2)}) copy-start(f32[1,3,4096]{2,0,1:T(1,128)} %copy-done.39) | copy-start | bytes 147460
  324.4 6.4 %copy-start.41 = (f32[1,3,4096]{2,0,1:T(1,128)S(1)}, f32[1,3,4096]{2,0,1:T(1,128)}, u32[]{:S(2)}) copy-start(f32[1,3,4096]{2,0,1:T(1,128)} %slice.802) | copy-start | bytes 147460
  330.8 0.8 copy-start.45
  330.8 0.8 copy-start.46
  359.3 1.2 copy-start.6
  359.3 1.2 copy-start.8
  371.1 3.5 copy-start.42
  379.6 2.9 copy-start.35
  379.6 2.9 copy-start.36
  379.7 3.0 copy-start.33
  379.7 3.0 copy-start.34
  379.9 2.9 copy-start.31
  379.9 3.0 copy-start.32
  381.2 1.8 copy-start.29
  381.2 1.8 copy-start.30
  383.2 1.9 copy-start.23
  383.2 1.9 copy-start.24
  394.3 105.2 %copy-start.10 = (f32[1,6,2,4096]{3,2,1,0:T(2,128)S(1)}, f32[1,6,2,4096]{3,2,1,0:T(2,128)}, u32[]{:S(2)}) copy-start(f32[1,6,2,4096]{3,2,1,0:T(2,128)} %get-tuple-element.220) | copy-start | bytes 589828
  394.3 107.0 %copy-start.11 = (f32[1,6,2,4096]{3,2,1,0:T(2,128)S(1)}, f32[1,6,2,4096]{3,2,1,0:T(2,128)}, u32[]{:S(2)}) copy-start(f32[1,6,2,4096]{3,2,1,0:T(2,128)} %get-tuple-element.219) | copy-start | bytes 589828
Sparse Core Ops, SparseCore 0:
  372.7 108.0 all-gather.2
where the time goes:
time: 579 us; the launch traced here: 568 us
  local copies, waits for them, and re-layouts  167 us (29%)
  other arithmetic  121 us (21%)
  waiting for transfers between devices  112 us (19%)
  blocking collectives  85.9 us (15%)
  matrix products  43 us (7%)
  starting transfers between devices  19.6 us (3%)
  between operations  19 us (3%)
    all_gather x1, waiting for transfers between devices, picked_2(): lax.all_gather(value, axis)  86.5 us
    reduce_sum x28, other arithmetic, colour_product(): return jnp.sum(left_matrix[:, :, None] * right_matrix[None, :, :], axis=1)  69.6 us
    unnamed x120, local copies, waits for them, and re-layouts  60.9 us
    psum x4, blocking collectives, over_axes(): value = lax.psum(value, axis)  52.4 us
    all_to_all x3, local copies, waits for them, and re-layouts, body(): lax.all_to_all(spectrum, SPACE, split_axis=3, concat_axis=2, tiled=True)  20.1 us
    all_gather x1, local copies, waits for them, and re-layouts, picked_2(): lax.all_gather(value, axis)  18.7 us
    another operation x6, local copies, waits for them, and re-layouts, body(): jnp.stack([real_six.reshape(6, planes, L * L), imag_six.reshape(6, planes...  17.9 us
    all_to_all x1, blocking collectives, body(): lax.all_to_all(widened, SPACE, split_axis=2, concat_axis=3, tiled=True)  16.9 us
  transfers between devices with their start and end apart: 5, of which 5 were waited for; matrix products, arithmetic and copies ran while one was open for 6% of the time, Pallas kernels for 0%

commit v1 on v0

v1 whole, which is shorter than its diff:
```python
import functools

import jax
import jax.numpy as jnp
import ml_dtypes
import numpy as np
from jax import lax
from jax.experimental import pallas as pl
from jax.experimental.pallas import tpu as pltpu
from jax.sharding import PartitionSpec as P

L = 64
SC = 12
ITERS = 2
STEP_SIZE = 0.08
PEAK_SQUARE = 12.0
ROWS = 32
PART = 24
SHARE = 24
F32 = jnp.float32
BF16 = jnp.bfloat16
MESH = pl.DeviceIdType.MESH


def halves(table):
    table = np.asarray(table, np.float32)
    high = table.astype(ml_dtypes.bfloat16)
    low = (table - high.astype(np.float32)).astype(ml_dtypes.bfloat16)
    return high, low


def left_table(table):
    high, low = halves(table)
    return np.concatenate([high, high, low], axis=1)


def right_table(table):
    high, low = halves(table)
    return np.concatenate([high, low], axis=0)


def tables(space_count):
    turn = 2.0 * np.pi
    short = np.arange(ROWS)
    angle = turn * (np.outer(short, short) % ROWS) / ROWS
    cosine, sine = np.cos(angle), np.sin(angle)
    row_forward = np.block([[cosine, sine], [-sine, cosine]])
    row_back = np.block([[cosine, -sine], [sine, cosine]])
    lane = np.arange(128)
    half, deep = lane // L, lane % L
    sign = np.where(np.outer(half, half) % 2 == 1, -1.0, 1.0)
    angle = turn * (np.outer(deep, deep) % L) / L
    cosine, sine = sign * np.cos(angle), sign * np.sin(angle)
    lane_forward = np.block([[cosine, -sine], [sine, cosine]])
    lane_back = np.block([[cosine, sine], [-sine, cosine]])
    angle = turn * np.outer(short, half) / L
    twist = np.stack([np.cos(angle), np.sin(angle)]).astype(np.float32)
    wave = np.arange(L)
    place = np.concatenate([(2 * np.arange(space_count) + plane) % L for plane in range(3)])
    angle = turn * (np.outer(wave, place) % L) / L
    cosine, sine = np.cos(angle), np.sin(angle)
    across_forward = np.block([[cosine, sine], [-sine, cosine]])
    across_back = np.block([[cosine.T, -sine.T], [sine.T, cosine.T]])
    square = 4.0 * np.sin(np.pi * wave / L) ** 2
    square_across = np.broadcast_to(square[:, None], (L, 128)).astype(np.float32)
    square_block = np.stack(
        [square[block + 32 * half] + square[deep] for block in range(space_count)]
    ).astype(np.float32)
    return (
        left_table(row_forward),
        left_table(row_back),
        right_table(lane_forward),
        right_table(lane_back),
        left_table(across_forward),
        left_table(across_back),
        twist,
        square_across,
        square_block[:, None, :],
    )


def dot(left, right):
    return lax.dot_general(left, right, (((1,), (0,)), ((), ())), preferred_element_type=F32)


def split(values):
    high = values.astype(BF16)
    return high, (values - high.astype(F32)).astype(BF16)


def table_times(table, values):
    high, low = split(values)
    return dot(table, jnp.concatenate([high, low, high], axis=0))


def times_table(values, table):
    size = table.shape[0] // 2
    high, low = split(values)
    upper = table[:size]
    return dot(high, upper) + dot(high, table[size:]) + dot(low, upper)


def c_mul(left, right):
    return (
        left[0] * right[0] - left[1] * right[1],
        left[0] * right[1] + left[1] * right[0],
    )


def matrix_product(left, right):
    out = []
    for row in range(3):
        line = []
        for column in range(3):
            real, imag = None, None
            for inner in range(3):
                lr, li = left[row][inner]
                rr, ri = right[inner][column]
                real_term = lr * rr - li * ri
                imag_term = lr * ri + li * rr
                real = real_term if real is None else real + real_term
                imag = imag_term if imag is None else imag + imag_term
            line.append((real, imag))
        out.append(line)
    return out


def product_dagger(left, right):
    turned = [[(right[c][r][0], -right[c][r][1]) for c in range(3)] for r in range(3)]
    out = []
    for row in range(3):
        line = []
        for column in range(3):
            real, imag = None, None
            for inner in range(3):
                lr, li = left[row][inner]
                rr, ri = right[column][inner]
                real_term = lr * rr + li * ri
                imag_term = li * rr - lr * ri
                real = real_term if real is None else real + real_term
                imag = imag_term if imag is None else imag + imag_term
            line.append((real, imag))
        out.append(line)
    del turned
    return out


def rotation_of(fields):
    x01, x02, x12 = (fields[0], fields[4]), (fields[1], fields[5]), (fields[2], fields[6])
    d0, d1 = fields[3], fields[7]
    d2 = -(d0 + d1)
    n01 = x01[0] * x01[0] + x01[1] * x01[1]
    n02 = x02[0] * x02[0] + x02[1] * x02[1]
    n12 = x12[0] * x12[0] + x12[1] * x12[1]
    s0, s1, s2 = d0 * d0, d1 * d1, d2 * d2
    t = -(0.5 * (s0 + s1 + s2) + (n01 + n02 + n12))
    pair = c_mul(x01, x12)
    imag_w = pair[1] * x02[0] - pair[0] * x02[1]
    e = d0 * n12 + d1 * n02 + d2 * n01 - d0 * d1 * d2 - 2.0 * imag_w
    y01 = (
        d2 * x01[1] - (x02[0] * x12[0] + x02[1] * x12[1]),
        -d2 * x01[0] - (x02[1] * x12[0] - x02[0] * x12[1]),
    )
    y02 = (d1 * x02[1] + pair[0], -d1 * x02[0] + pair[1])
    y12 = (
        d0 * x12[1] - (x01[0] * x02[0] + x01[1] * x02[1]),
        -d0 * x12[0] - (x01[0] * x02[1] - x01[1] * x02[0]),
    )
    q0, q1, q2 = -(s0 + n01 + n02), -(s1 + n01 + n12), -(s2 + n02 + n12)
    a = (jnp.ones_like(t), e * (1.0 / 120.0))
    b = ((1.0 + t * (1.0 / 30.0)) * 0.25, jnp.zeros_like(t))
    c = (jnp.full_like(t, 0.05), jnp.zeros_like(t))
    for degree in (3, 2, 1):
        scale = 1.0 / degree
        a, b, c = (
            (1.0 - e * c[1] * scale, e * c[0] * scale),
            ((a[0] + c[0] * t) * scale, (a[1] + c[1] * t) * scale),
            (b[0] * scale, b[1] * scale),
        )
    for _ in range(3):
        aa, bb, cc = c_mul(a, a), c_mul(b, b), c_mul(c, c)
        ab, ac, bc = c_mul(a, b), c_mul(a, c), c_mul(b, c)
        a, b, c = (
            (aa[0] - 2.0 * e * bc[1], aa[1] + 2.0 * e * bc[0]),
            (
                2.0 * (ab[0] + t * bc[0]) - e * cc[1],
                2.0 * (ab[1] + t * bc[1]) + e * cc[0],
            ),
            (2.0 * ac[0] + bb[0] + t * cc[0], 2.0 * ac[1] + bb[1] + t * cc[1]),
        )
    out = [[None] * 3 for _ in range(3)]
    for at, (d, q) in enumerate(((d0, q0), (d1, q1), (d2, q2))):
        out[at][at] = (a[0] - b[1] * d + c[0] * q, a[1] + b[0] * d + c[1] * q)
    for row, column, x, y in ((0, 1, x01, y01), (0, 2, x02, y02), (1, 2, x12, y12)):
        p1, p2, p3, p4 = b[0] * x[0], b[1] * x[1], b[0] * x[1], b[1] * x[0]
        r1, r2, r3, r4 = c[0] * y[0], c[1] * y[1], c[0] * y[1], c[1] * y[0]
        out[row][column] = (p1 - p2 + r1 - r2, p3 + p4 + r3 + r4)
        out[column][row] = (r1 + r2 - p1 - p2, p3 - p4 - r3 + r4)
    return out


def entry(row, column):
    return row * 3 + column


def kernel(
    space_count,
    time_count,
    sink_time,
    src_time,
    src_site,
    links_in,
    prop_in,
    row_forward,
    row_back,
    lane_forward,
    lane_back,
    across_forward,
    across_back,
    twist,
    square_across,
    square_block,
    links_out,
    rows_out,
    lk,
    pr,
    send,
    recv,
    algebra,
    gauge,
    ahead_y,
    half_in,
    stage,
    share_in,
    shared,
    full,
    lines,
    line,
    line_in,
    total_line,
    total_in,
    copy_sem,
    a2a_send,
    a2a_recv,
    half_sem,
    one_send,
    one_recv,
    two_send,
    two_recv,
    swap_sem,
    line_send,
    line_recv,
    last_send,
    last_recv,
):
    me = lax.axis_index("space")
    my_time = lax.axis_index("tm")
    depth_count = time_count // 2
    my_depth = my_time // 2
    my_core = my_time % 2
    partner = my_time + 1 - 2 * my_core
    sink_slice = lax.rem(sink_time[0], time_count)
    source_slice = lax.rem(src_time[0], time_count)
    sink_depth = sink_slice // 2
    sink_core = sink_slice - 2 * sink_depth

    load_links = pltpu.make_async_copy(links_in, lk, copy_sem.at[0])
    load_links.start()
    load_prop = pltpu.make_async_copy(prop_in, pr, copy_sem.at[1])
    load_prop.start()

    barrier = pltpu.get_barrier_semaphore()

    def greet_space(step, carry):
        peer = lax.rem(me + step, space_count)
        pl.semaphore_signal(barrier, inc=1, device_id={"space": peer}, device_id_type=MESH)
        return carry

    def greet_time(step, carry):
        peer = lax.rem(my_time + step, time_count)
        pl.semaphore_signal(barrier, inc=1, device_id={"tm": peer}, device_id_type=MESH)
        return carry

    lax.fori_loop(1, space_count, greet_space, 0)
    lax.fori_loop(1, time_count, greet_time, 0)

    lane_at = lax.broadcasted_iota(jnp.int32, (ROWS, 128), 1)
    row_at = lax.broadcasted_iota(jnp.int32, (ROWS, 128), 0)
    first_half = lane_at < L
    deep_at = lane_at % L
    deep_chunk = lax.broadcasted_iota(jnp.int32, (8, 128), 1) % L
    deep_last = deep_chunk == L - 1

    def from_lower_y(values):
        turned = pltpu.roll(values, L, 1)
        return jnp.where(first_half, pltpu.roll(turned, 1, 0), turned)

    def from_upper_y(values):
        turned = pltpu.roll(values, L, 1)
        return jnp.where(first_half, turned, pltpu.roll(turned, ROWS - 1, 0))

    def from_lower_z(values):
        return jnp.where(deep_at == 0, pltpu.roll(values, L + 1, 1), pltpu.roll(values, 1, 1))

    def chunk_upper_z(values):
        return jnp.where(deep_last, pltpu.roll(values, L - 1, 1), pltpu.roll(values, 127, 1))

    def projected(direction, plane):
        def one(part, row, column):
            start = ((direction * 2 + part) * 9 + entry(row, column)) * L + plane
            return lk[pl.ds(start, ROWS, stride=2), :]

        real, imag = [], []
        for row, column in ((0, 1), (0, 2), (1, 2)):
            real.append(0.5 * (one(0, row, column) - one(0, column, row)))
            imag.append(0.5 * (one(1, row, column) + one(1, column, row)))
        diagonal = [one(1, at, at) for at in range(3)]
        third = (diagonal[0] + diagonal[1] + diagonal[2]) * (1.0 / 3.0)
        real.append(diagonal[0] - third)
        imag.append(diagonal[1] - third)
        return real + imag

    def exchange(round_index, step):
        peer = lax.rem(me + step, space_count)
        return pltpu.make_async_remote_copy(
            src_ref=send.at[round_index, pl.ds(pl.multiple_of(peer * PART, 8), PART), :],
            dst_ref=recv.at[round_index, pl.ds(pl.multiple_of(me * PART, 8), PART), :],
            send_sem=a2a_send.at[round_index, step],
            recv_sem=a2a_recv.at[round_index, me],
            device_id={"space": peer},
            device_id_type=MESH,
        )

    def exchange_arrival(round_index, step):
        peer = lax.rem(me + step, space_count)
        return pltpu.make_async_remote_copy(
            src_ref=send.at[round_index, pl.ds(pl.multiple_of(peer * PART, 8), PART), :],
            dst_ref=recv.at[round_index, pl.ds(pl.multiple_of(peer * PART, 8), PART), :],
            send_sem=a2a_send.at[round_index, step],
            recv_sem=a2a_recv.at[round_index, peer],
            device_id={"space": peer},
            device_id_type=MESH,
        )

    def start_exchange(round_index):
        def begin(step, carry):
            exchange(round_index, step).start()
            return carry

        lax.fori_loop(1, space_count, begin, 0)
        own = pl.ds(pl.multiple_of(me * PART, 8), PART)
        recv[round_index, own, :] = send[round_index, own, :]

    def end_exchange(round_index):
        def finish(step, carry):
            arrival = exchange_arrival(round_index, step)
            arrival.wait_send()
            arrival.wait_recv()
            return carry

        lax.fori_loop(1, space_count, finish, 0)

    def block_rows(plane, part, field):
        return pl.ds(plane * 8 + part * 4 + field, space_count, stride=PART)

    def spread(sweep):
        nothing = [jnp.zeros((ROWS, 128), F32)] * 8
        fields = []
        along_x = [projected(0, plane) for plane in range(2)]
        for plane in range(2):
            along_y, along_z = projected(1, plane), projected(2, plane)
            behind = nothing if plane == 0 else along_x[0]
            fields.append(
                [
                    behind[at]
                    - along_x[plane][at]
                    + (from_lower_y(along_y[at]) - along_y[at])
                    + (from_lower_z(along_z[at]) - along_z[at])
                    for at in range(8)
                ]
            )
        fields.append(along_x[1])
        wide = [
            jnp.concatenate(
                [fields[plane][part * 4 + at] for plane in range(3) for at in range(4)], axis=1
            )
            for part in range(2)
        ]
        turned = table_times(row_forward[...], jnp.concatenate(wide, axis=0))
        cosine, sine = twist[0], twist[1]
        lines_in = []
        for block in range(12):
            real = turned[:ROWS, block * 128 : (block + 1) * 128]
            imag = turned[ROWS:, block * 128 : (block + 1) * 128]
            lines_in.append(
                jnp.concatenate([real * cosine + imag * sine, imag * cosine - real * sine], axis=1)
            )
        spectrum = times_table(jnp.concatenate(lines_in, axis=0), lane_forward)
        for plane in range(3):
            for part in range(2):
                for field in range(4):
                    at = (plane * 4 + field) * ROWS
                    send[2 * sweep, block_rows(plane, part, field), :] = spectrum[
                        at : at + ROWS, part * 128 : (part + 1) * 128
                    ]

    def across(sweep):
        gathered = jnp.concatenate(
            [
                jnp.concatenate(
                    [recv[2 * sweep, block_rows(plane, part, field), :] for field in range(4)],
                    axis=1,
                )
                for part in range(2)
                for plane in range(3)
            ],
            axis=0,
        )
        spectrum = table_times(across_forward[...], gathered)
        momentum = square_across[...] + square_block[me]
        inside = momentum > 0.0
        factor = PEAK_SQUARE * (STEP_SIZE / 16.0) / float(L) ** 3
        weight = jnp.where(inside, factor / jnp.where(inside, momentum, 1.0), 0.0)
        weight = jnp.concatenate([jnp.concatenate([weight] * 4, axis=1)] * 2, axis=0)
        back = table_times(across_back[...], spectrum * weight)
        for part in range(2):
            for plane in range(3):
                for field in range(4):
                    at = (part * 3 + plane) * ROWS
                    send[2 * sweep + 1, block_rows(plane, part, field), :] = back[
                        at : at + ROWS, field * 128 : (field + 1) * 128
                    ]

    def algebra_rows(plane, part, field):
        if plane == 2:
            return 512 + (part * 4 + field) * ROWS
        return part * 256 + (plane * 4 + field) * ROWS

    def gather_back(sweep):
        lines_in = jnp.concatenate(
            [
                jnp.concatenate(
                    [recv[2 * sweep + 1, block_rows(plane, part, field), :] for part in range(2)],
                    axis=1,
                )
                for plane in range(3)
                for field in range(4)
            ],
            axis=0,
        )
        turned = times_table(lines_in, lane_back)
        cosine, sine = twist[0], twist[1]
        reals, imags = [], []
        for block in range(12):
            real = turned[block * ROWS : (block + 1) * ROWS, :128]
            imag = turned[block * ROWS : (block + 1) * ROWS, 128:]
            reals.append(real * cosine - imag * sine)
            imags.append(imag * cosine + real * sine)
        wide = jnp.concatenate(
            [jnp.concatenate(reals, axis=1), jnp.concatenate(imags, axis=1)], axis=0
        )
        sites = table_times(row_back[...], wide)
        for plane in range(3):
            for part in range(2):
                for field in range(4):
                    block = plane * 4 + field
                    start = algebra_rows(plane, part, field)
                    algebra[sweep, start : start + ROWS, :] = sites[
                        part * ROWS : (part + 1) * ROWS, block * 128 : (block + 1) * 128
                    ]

    def exponentials(sweep):
        def one(step, carry):
            plane, row = step // 4, pl.multiple_of((step % 4) * 8, 8)
            base = jnp.where(plane == 2, 512, plane * 128)
            stride = jnp.where(plane == 2, 128, 256)
            fields = []
            for part in range(2):
                for field in range(4):
                    start = pl.multiple_of(base + part * stride + field * ROWS + row, 8)
                    fields.append(algebra[sweep, pl.ds(start, 8), :])
            matrix = rotation_of(fields)
            for part in range(2):
                for a in range(3):
                    for b in range(3):
                        gauge[plane, part * 9 + entry(a, b), pl.ds(row, 8), :] = matrix[a][b][part]
            return carry

        lax.fori_loop(0, 12, one, 0)

        def shift(plane, carry):
            for at in range(18):
                ahead_y[plane, at] = from_upper_y(gauge[plane, at])
            return carry

        lax.fori_loop(0, 2, shift, 0)

    def matrix_at(read):
        return [[(read(entry(a, b)), read(9 + entry(a, b))) for b in range(3)] for a in range(3)]

    def rotate_links():
        def one(step, carry):
            plane, chunk = step // 4, step % 4
            row = pl.multiple_of(chunk * 8, 8)
            here = matrix_at(lambda at: gauge[plane, at, pl.ds(row, 8), :])
            for direction in range(3):
                if direction == 0:
                    ahead = matrix_at(lambda at: gauge[plane + 1, at, pl.ds(row, 8), :])
                elif direction == 1:
                    ahead = matrix_at(lambda at: ahead_y[plane, at, pl.ds(row, 8), :])
                else:
                    ahead = [[tuple(chunk_upper_z(v) for v in pair) for pair in r] for r in here]

                def rows(at):
                    start = (direction * 18 + at) * L
                    return pl.ds(start + 16 * chunk + plane, 8, stride=2)

                link = matrix_at(lambda at: lk[rows(at), :])
                moved = product_dagger(matrix_product(here, link), ahead)
                for part in range(2):
                    for a in range(3):
                        for b in range(3):
                            lk[rows(part * 9 + entry(a, b)), :] = moved[a][b][part]
            return carry

        lax.fori_loop(0, 8, one, 0)

    plane_index = src_site[0] // (L * L) - 2 * me
    column_index = lax.rem(src_site[0], L * L)
    wanted = jnp.where(source_slice == my_time, plane_index * (L * L) + column_index, -1)

    def anchor_lines(sweep):
        site = row_at * 128 + lane_at
        for at in range(18):
            picked = jnp.where(site == wanted, gauge[0, at], 0.0) + jnp.where(
                site + L * L == wanted, gauge[1, at], 0.0
            )
            place = 12 + 18 * sweep + at
            lines[place : place + 1, :] = jnp.sum(picked, axis=0, keepdims=True)

    def half_copy(sweep):
        return pltpu.make_async_remote_copy(
            src_ref=algebra.at[sweep, pl.ds(pl.multiple_of((1 - my_core) * 256, 8), 256), :],
            dst_ref=half_in.at[sweep],
            send_sem=half_sem.at[sweep, 0],
            recv_sem=half_sem.at[sweep, 1],
            device_id={"tm": partner},
            device_id_type=MESH,
        )

    def share_copy(sweep, step, arrival):
        depth = lax.rem(my_depth + step, depth_count)
        landing = depth if arrival else my_depth
        return pltpu.make_async_remote_copy(
            src_ref=stage.at[sweep, depth],
            dst_ref=share_in.at[sweep, landing],
            send_sem=one_send.at[sweep, step],
            recv_sem=one_recv.at[sweep, landing],
            device_id={"tm": depth * 2 + my_core},
            device_id_type=MESH,
        )

    def shared_copy(sweep, step, arrival):
        depth = lax.rem(my_depth + step, depth_count)
        landing = depth if arrival else my_depth
        return pltpu.make_async_remote_copy(
            src_ref=shared.at[sweep],
            dst_ref=full.at[sweep, my_core, landing],
            send_sem=two_send.at[sweep, step],
            recv_sem=two_recv.at[sweep, landing],
            device_id={"tm": depth * 2 + my_core},
            device_id_type=MESH,
        )

    def swap_copy(sweep, arrival):
        core = 1 - my_core if arrival else my_core
        return pltpu.make_async_remote_copy(
            src_ref=full.at[sweep, my_core],
            dst_ref=full.at[sweep, core],
            send_sem=swap_sem.at[sweep, 0],
            recv_sem=swap_sem.at[sweep, 1],
            device_id={"tm": partner},
            device_id_type=MESH,
        )

    def each_depth(action):
        def one(step, carry):
            action(step)
            return carry

        lax.fori_loop(1, depth_count, one, 0)

    def sink_start(sweep):
        half_copy(sweep).start()

    def sink_shares(sweep):
        half_copy(sweep).wait()
        mine = algebra[sweep, pl.ds(pl.multiple_of(my_core * 256, 8), 256), :]
        chosen = jnp.where(sink_core == my_core, mine, half_in[sweep])
        for at in range(depth_count):
            low, high = at * SHARE, min((at + 1) * SHARE, 256)
            if high > low:
                stage[sweep, at, : high - low, :] = chosen[low:high]
            filled = max(high - low, 0)
            if filled < SHARE:
                stage[sweep, at, filled:, :] = jnp.zeros((SHARE - filled, 128), F32)
        each_depth(lambda step: share_copy(sweep, step, False).start())
        share_in[sweep, my_depth] = stage[sweep, my_depth]

    def wait_both(copy):
        copy.wait_send()
        copy.wait_recv()

    def sink_shared(sweep):
        each_depth(lambda step: wait_both(share_copy(sweep, step, True)))
        value = share_in[sweep, sink_depth]
        shared[sweep] = value
        full[sweep, my_core, my_depth] = value
        each_depth(lambda step: shared_copy(sweep, step, False).start())

    def sink_swap(sweep):
        each_depth(lambda step: wait_both(shared_copy(sweep, step, True)))
        swap_copy(sweep, False).start()

    def sink_end(sweep):
        copy = swap_copy(sweep, True)
        copy.wait_send()
        copy.wait_recv()

    def sink_sum():
        def one(step, sums):
            plane, chunk = step // 4, step % 4

            def rotation(sweep):
                fields = []
                for part in range(2):
                    for field in range(4):
                        tile = (plane * 4 + field) * 4 + chunk
                        fields.append(
                            full[
                                sweep,
                                part,
                                tile // 3,
                                pl.ds(pl.multiple_of(lax.rem(tile, 3) * 8, 8), 8),
                                :,
                            ]
                        )
                return rotation_of(fields)

            total = matrix_product(rotation(1), rotation(0))

            def source(part, pair):
                return pr[pl.ds((part * 6 + pair) * L + 16 * chunk + plane, 8, stride=2), :]

            out = list(sums)
            for group in range(2):
                column = [(source(0, group * 3 + c), source(1, group * 3 + c)) for c in range(3)]
                for a in range(3):
                    at = group * 3 + a
                    for c in range(3):
                        real, imag = c_mul(total[a][c], column[c])
                        out[at] = out[at] + real
                        out[6 + at] = out[6 + at] + imag
            return tuple(out)

        zero = jnp.zeros((8, 128), F32)
        sums = lax.fori_loop(0, 8, one, (zero,) * 12)
        for at in range(12):
            lines[at : at + 1, :] = jnp.sum(sums[at], axis=0, keepdims=True)

    def line_copy(step, arrival):
        peer = lax.rem(me + step, space_count)
        landing = peer if arrival else me
        return pltpu.make_async_remote_copy(
            src_ref=line,
            dst_ref=line_in.at[landing],
            send_sem=line_send.at[step],
            recv_sem=line_recv.at[landing],
            device_id={"space": peer},
            device_id_type=MESH,
        )

    def total_copy(step, arrival):
        peer = lax.rem(my_time + step, time_count)
        landing = peer if arrival else my_time
        return pltpu.make_async_remote_copy(
            src_ref=total_line,
            dst_ref=total_in.at[landing],
            send_sem=last_send.at[step],
            recv_sem=last_recv.at[landing],
            device_id={"tm": peer},
            device_id_type=MESH,
        )

    def over(count, action):
        def one(step, carry):
            action(step)
            return carry

        lax.fori_loop(1, count, one, 0)

    load_links.wait()
    spread(0)
    pl.semaphore_wait(barrier, space_count + time_count - 2)
    start_exchange(0)
    end_exchange(0)
    across(0)
    start_exchange(1)
    end_exchange(1)
    gather_back(0)
    sink_start(0)
    exponentials(0)
    rotate_links()
    spread(1)
    start_exchange(2)
    sink_shares(0)
    anchor_lines(0)
    end_exchange(2)
    across(1)
    start_exchange(3)
    sink_shared(0)
    end_exchange(3)
    gather_back(1)
    sink_start(1)
    sink_swap(0)
    exponentials(1)
    sink_shares(1)
    rotate_links()
    store_links = pltpu.make_async_copy(lk, links_out, copy_sem.at[0])
    store_links.start()
    sink_shared(1)
    anchor_lines(1)
    load_prop.wait()
    sink_end(0)
    sink_swap(1)
    sink_end(1)
    sink_sum()
    values = jnp.sum(lines[...], axis=1, keepdims=True)
    diagonal = lax.broadcasted_iota(jnp.int32, (48, 128), 0) == lax.broadcasted_iota(
        jnp.int32, (48, 128), 1
    )
    mine = jnp.sum(jnp.where(diagonal, values, 0.0), axis=0, keepdims=True)
    line[...] = mine
    over(space_count, lambda step: line_copy(step, False).start())
    line_in[me] = mine
    over(space_count, lambda step: wait_both(line_copy(step, True)))
    summed = jnp.sum(line_in[...], axis=0)
    total_line[...] = summed
    over(time_count, lambda step: total_copy(step, False).start())
    total_in[my_time] = summed
    over(time_count, lambda step: wait_both(total_copy(step, True)))
    rows_out[...] = total_in[...]
    store_links.wait()


def complex_matrix(parts):
    return parts.reshape(2, 3, 3)


def body(space_count, time_count, links, propagator, sink_time, src_time, src_site):
    planes = links.shape[5]

    def dense(values, count):
        folded = values.reshape(count, planes, ROWS, 128).transpose(0, 2, 1, 3)
        return folded.reshape(count * planes * ROWS, 128)

    link_rows = dense(links, 54)
    prop_rows = dense(propagator, 12)
    constants = [jnp.asarray(table) for table in tables(space_count)]
    smem = pl.BlockSpec(memory_space=pltpu.SMEM)
    vmem = pl.BlockSpec(memory_space=pltpu.VMEM)
    anywhere = pl.BlockSpec(memory_space=pl.ANY)
    dma = pltpu.SemaphoreType.DMA
    depth_count = time_count // 2
    fixed_rows, rows = pl.pallas_call(
        functools.partial(kernel, space_count, time_count),
        out_shape=(
            jax.ShapeDtypeStruct(link_rows.shape, F32),
            jax.ShapeDtypeStruct((time_count, 1, 128), F32),
        ),
        in_specs=[smem] * 3 + [anywhere] * 2 + [vmem] * 9,
        out_specs=(anywhere, vmem),
        scratch_shapes=[
            pltpu.VMEM(link_rows.shape, F32),
            pltpu.VMEM(prop_rows.shape, F32),
            pltpu.VMEM((4, space_count * PART, 128), F32),
            pltpu.VMEM((4, space_count * PART, 128), F32),
            pltpu.VMEM((2, 768, 128), F32),
            pltpu.VMEM((3, 18, ROWS, 128), F32),
            pltpu.VMEM((2, 18, ROWS, 128), F32),
            pltpu.VMEM((2, 256, 128), F32),
            pltpu.VMEM((2, depth_count, SHARE, 128), F32),
            pltpu.VMEM((2, depth_count, SHARE, 128), F32),
            pltpu.VMEM((2, SHARE, 128), F32),
            pltpu.VMEM((2, 2, depth_count, SHARE, 128), F32),
            pltpu.VMEM((48, 128), F32),
            pltpu.VMEM((1, 128), F32),
            pltpu.VMEM((space_count, 1, 128), F32),
            pltpu.VMEM((1, 128), F32),
            pltpu.VMEM((time_count, 1, 128), F32),
            dma((2,)),
            dma((4, space_count)),
            dma((4, space_count)),
            dma((2, 2)),
            dma((2, depth_count)),
            dma((2, depth_count)),
            dma((2, depth_count)),
            dma((2, depth_count)),
            dma((2, 2)),
            dma((space_count,)),
            dma((space_count,)),
            dma((time_count,)),
            dma((time_count,)),
        ],
        compiler_params=pltpu.CompilerParams(
            collective_id=0, has_side_effects=True, vmem_limit_bytes=48 * 1024 * 1024
        ),
    )(sink_time, src_time, src_site, link_rows, prop_rows, *constants)
    fixed = fixed_rows.reshape(54, ROWS, planes, 128).transpose(0, 2, 1, 3).reshape(links.shape)
    rows = rows.reshape(time_count, 128)
    sums = rows[:, :SC].reshape(time_count, 2, 6).transpose(1, 0, 2).reshape(2, 4, 3, SC)
    anchors = jnp.sum(rows[:, SC : SC + 36], axis=0)
    first, second = complex_matrix(anchors[:18]), complex_matrix(anchors[18:])

    def product(left, right):
        return jnp.sum(left[:, :, None] * right[None, :, :], axis=1)

    real = product(second[0], first[0]) - product(second[1], first[1])
    imag = product(second[0], first[1]) + product(second[1], first[0])

    def rotated(values, matrix):
        return jnp.sum(values[:, None] * matrix[None, :, :, None], axis=2)

    wall = jnp.stack(
        [
            rotated(sums[0], real) + rotated(sums[1], imag),
            rotated(sums[1], real) - rotated(sums[0], imag),
        ]
    ).reshape(2, SC * SC)
    return fixed, wall * float(planes * space_count * L * L) ** (-0.5)


def solution(mesh):
    placed = (
        P("tm", None, None, None, None, "space", None),
        P(None, "tm", "space", None),
        P(),
        P(),
        P(),
    )
    return jax.shard_map(
        functools.partial(body, mesh.shape["space"], mesh.shape["tm"]),
        mesh=mesh,
        in_specs=placed,
        out_specs=(P("tm", None, None, None, None, "space", None), P()),
        check_vma=False,
    )
```

time: 579 us -> 128 us (0.22); the launches traced: 568 us -> 127 us
  local copies, waits for them, and re-layouts: 167 us -> 12.2 us
  other arithmetic: 121 us -> 0.9 us
  Pallas kernels: 0 us -> 112 us
  waiting for transfers between devices: 112 us -> 0 us
  blocking collectives: 85.9 us -> 0 us
  matrix products: 43 us -> 0 us
  starting transfers between devices: 19.6 us -> 0 us
  between operations: 19 us -> 2.67 us
    pallas_call x0 -> x1, Pallas kernels: none -> 112 us  [body(): pl.pallas_call(functools.partial(kernel, space_count, time_count), out_sh...]
    all_gather x1 -> x0, waiting for transfers between devices: 86.5 us -> none  [picked_2(): lax.all_gather(value, axis)]
    reduce_sum x28 -> x3, other arithmetic: 69.6 us -> 0.29 us  [the longest x1 0.1 us: rotated(): return jnp.sum(values[:, None] * matrix[None, :, :, None], axis=2)]
    psum x4 -> x0, blocking collectives: 52.4 us -> none  [over_axes(): value = lax.psum(value, axis)]
    unnamed x120 -> x23, local copies, waits for them, and re-layouts: 60.9 us -> 11.1 us
    dot_general x56 -> x0, matrix products: 43 us -> none  [the longest x12 9.17 us: transform(): sine_real = jnp.einsum(pattern, sine_table, real_part, precision=EXACT)]
    all_to_all x2 -> x0, blocking collectives: 33.5 us -> none  [the longest x1 16.9 us: body(): lax.all_to_all(widened, SPACE, split_axis=2, concat_axis=3, tiled=True)]
    another operation x38 -> x0, local copies, waits for them, and re-layouts: 23.8 us -> none  [the longest x6 17.9 us: body(): jnp.stack([real_six.reshape(6, planes, L * L), imag_six.reshape(6, planes...]
  transfers between devices with their start and end apart: 5 -> 0, of which waited for: 5 -> 0; matrix products, arithmetic and copies ran while one was open for 6% -> 0% of each run, Pallas kernels for 0% -> 0%
where the time goes in v1:
time: 128 us; the launch traced here: 127 us
  Pallas kernels  112 us (88%)
  local copies, waits for them, and re-layouts  12.2 us (10%)
  between operations  2.67 us (2%)
    pallas_call x1, Pallas kernels, body(): pl.pallas_call(functools.partial(kernel, space_count, time_count), out_sh...  112 us
    unnamed x23, local copies, waits for them, and re-layouts  11.1 us

profile of v1, /device:TPU:1, one launch (start us, length us, event | category | flops | bytes accessed | tf_op | source)
XLA Modules:
  0.0 127.3 jit_solution(8766122678341568699)
XLA Ops:
  2.6 0.0 copy-start
  2.6 1.5 %copy-done = f32[1,3,2,3,3,2,4096]{6,5,4,3,2,1,0:T(2,128)S(1)} copy-done((f32[1,3,2,3,3,2,4096]{6,5,4,3,2,1,0:T(2,128)S(1)}, f32[1,3,2,3,3,2,4096]{6,5,4,3,2,1,0:T(2,128)}, u32[]{:S(2)}) %copy-start) | copy-done | bytes 1769496
  4.0 0.0 copy-start.1
  4.0 1.0 copy-done.1
  5.0 0.0 copy-start.2
  5.0 0.9 copy-done.2
  6.0 0.0 copy-start.3
  6.0 0.9 copy-done.3
  6.9 0.0 copy-start.4
  6.9 0.9 copy-done.4
  7.9 0.0 copy-start.5
  7.9 0.9 copy-done.5
  8.8 0.0 copy-start.6
  8.8 0.8 copy-done.6
  9.5 0.0 copy-start.7
  9.5 0.8 copy-done.7
  10.3 0.0 copy-start.8
  10.3 0.8 copy-done.8
  11.0 0.0 copy-start.9
  11.0 0.8 copy-done.9
  11.8 0.0 copy-start.10
  11.8 0.7 copy-done.10
  12.5 111.6 %shard_map.149 = (f32[3456,128]{1,0:T(8,128)S(1)}, f32[24,1,128]{2,1,0:T(1,128)S(1)}) custom-call(s32[1]{0:T(128)S(6)} %copy.36.sink_time, s32[1]{0:T(128)S(6)} %copy.37.src_time, s32[1]{0:T(128)S(6)} %copy.38.src_site, f32[3456,128]{1,0:T(8,128)S(1)} %bitcast.20, f32[768,128]{1,0:T(8,128)S(1)} %bitcast.22, bf16[64,192]{1,0:T(8,128)(2,1)S(1)} %copy-done.6, ...), custom_call_target="tpu_custom_call" | custom-call | tf_op jit(solution)/shard_map/pallas_call | solution.py:775
  124.1 0.1 slice_reduce_fusion
  124.2 0.1 fusion.1
  124.3 0.1 mul.50
  124.4 0.1 mul.52
  124.5 0.1 mul.55
  124.6 0.1 mul.57
  124.6 0.1 multiply_reduce_fusion.4
  124.8 0.1 copy.28
  124.9 0.1 copy.29
  124.9 0.1 mul.48
  125.0 0.1 copy.31
  125.1 0.1 mul.120
  125.2 0.1 multiply_reduce_fusion.3
  125.3 0.1 add.23
  125.4 0.1 sub.23
  125.5 0.6 maximum_multiply_fusion
  126.1 1.2 copy.39
  (10 shorter events, 0.1 us)
Async XLA Ops:
  2.6 1.5 %copy-start = (f32[1,3,2,3,3,2,4096]{6,5,4,3,2,1,0:T(2,128)S(1)}, f32[1,3,2,3,3,2,4096]{6,5,4,3,2,1,0:T(2,128)}, u32[]{:S(2)}) copy-start(f32[1,3,2,3,3,2,4096]{6,5,4,3,2,1,0:T(2,128)} %param.14) | copy-start | bytes 5308420
  4.0 1.0 copy-start.1
  5.0 0.9 copy-start.2
  6.0 0.9 copy-start.3
  6.9 0.9 copy-start.4
  7.9 0.9 copy-start.5
  8.8 0.8 copy-start.6
  9.5 0.8 copy-start.7
  10.3 0.8 copy-start.8
  11.0 0.8 copy-start.9
  11.8 0.7 copy-start.10
